TPU v7x, 32 devices: a whole 2x2x4 slice. The times are simulated.
32 devices in a mesh: expert: 2 (over y), dp: 4 (over x, core), shard: 4 (over z).
Axes of the slice: x: 2, y: 2, z: 4, core: 2. Of those that a mesh axis runs over, the one named last changes fastest.
Arguments:
- grad_partials: bfloat16 [4, 2, 4096, 1536], P('dp', 'expert', 'shard'), may hold values from -120 to 120
- momentum: float32 [2, 4, 1024, 1536], P('expert', 'shard', 'dp'), may hold values from -3 to 3
- q_factor: float32 [1536, 2, 384], P(('dp', 'shard'), 'expert'), may hold values from -0.15625 to 0.15625
Outputs:
- next_momentum: float32 [2, 4, 1024, 1536], P('expert', 'shard', 'dp')
- next_factor: float32 [1536, 2, 384], P(('dp', 'shard'), 'expert')
- weight_update: bfloat16 [2, 4096, 1536], P('expert', 'shard')
All inputs are finite; a program needn't handle non-finite values.
Results may differ from a plain program's by a relative error of at most 0.015.
Values may be sent and summed in bfloat16 or wider, within the bound.
A program may use at most 64 MiB of HBM per device.

v0:
```python
import math
import jax
import jax.numpy as jnp
from jax import lax
from jax.sharding import PartitionSpec as P

clip_rms = 0.5
keep_share = 0.95
highest = lax.Precision.HIGHEST


def orthonormal(projected):
    gram_matrix = lax.psum(
        jnp.einsum("emr,ems->ers", projected, projected, precision=highest), ("dp", "shard")
    )
    triangles = jnp.linalg.cholesky(gram_matrix)

    def solve_one(triangle, columns):
        return jax.scipy.linalg.solve_triangular(triangle, columns.T, lower=True).T

    return jax.vmap(solve_one)(triangles, projected)


def shards(grad_partials, momentum, q_factor):
    partial_value = grad_partials[0]
    gradient = lax.psum_scatter(partial_value, "dp", scatter_dimension=1, tiled=True).astype(
        jnp.float32
    )
    momentum_rows = momentum[:, 0]
    experts, local_rows, hidden_width = gradient.shape
    factor_count, _, rank_width = q_factor.shape
    total_rows = local_rows * lax.axis_size("dp") * lax.axis_size("shard")
    entries = float(experts * lax.axis_size("expert") * total_rows * hidden_width)
    square_sum = lax.psum(jnp.sum(gradient * gradient), ("expert", "dp", "shard"))
    clip_scale = clip_rms / jnp.sqrt(square_sum / entries + 1e-06)
    buffer = momentum_rows + clip_scale * gradient
    zeros_init = jnp.zeros((experts, local_rows, rank_width), jnp.float32)
    projected = zeros_init + jnp.einsum(
        "emf,fer->emr",
        buffer,
        lax.all_gather(q_factor.astype(jnp.bfloat16), ("dp", "shard"), axis=0, tiled=True).astype(
            jnp.float32
        ),
        precision=highest,
    )
    ortho_basis = orthonormal(projected)
    right_term = jnp.einsum("emf,emr->fer", buffer, ortho_basis, precision=highest)
    right_factor = lax.psum(right_term, ("dp", "shard"))
    inverse = lax.rsqrt(jnp.sum(right_factor * right_factor, axis=0) + 1e-06)
    offset = (
        lax.axis_index("dp") * lax.axis_size("shard") + lax.axis_index("shard")
    ) * factor_count
    next_factor = lax.dynamic_slice_in_dim(right_factor, offset, factor_count, 0) * inverse[None]
    correction = jnp.einsum("emr,fer->emf", ortho_basis, right_factor, precision=highest)
    direction = jnp.einsum(
        "emr,fer->emf", ortho_basis * inverse[:, None, :], right_factor, precision=highest
    )
    next_momentum = (buffer - (1.0 - keep_share) * correction)[:, None]
    unit_scale = math.sqrt(total_rows * hidden_width / rank_width)
    local_update = (unit_scale * direction).astype(jnp.bfloat16)
    weight_update = lax.all_gather(local_update, "dp", axis=1, tiled=True)
    return (next_momentum, next_factor, weight_update)


def solution(mesh):
    placed = (
        P("dp", "expert", "shard", None),
        P("expert", "shard", "dp", None),
        P(("dp", "shard"), "expert", None),
    )
    return jax.shard_map(
        shards,
        mesh=mesh,
        in_specs=placed,
        out_specs=(
            P("expert", "shard", "dp", None),
            P(("dp", "shard"), "expert", None),
            P("expert", "shard", None),
        ),
        check_vma=False,
    )
```

profile of v0, /device:TPU:0, one launch (start us, length us, event | category | flops | bytes accessed | tf_op | source)
XLA Modules:
  0.0 446.0 jit_solution(1453472707407732005)
XLA Ops:
  8.0 0.0 reduce-scatter.2.cloned.1.call-start
  8.0 0.0 copy-start.5
  8.1 0.0 copy-start.1
  8.1 0.7 reduce-scatter.2.cloned.1.call-update
  8.7 0.0 all-gather.4.cloned.1.call-start
  8.8 0.2 copy-done.5
  9.0 0.6 copy.21
  9.6 0.0 all-gather.4.cloned.1.call-update
  9.6 0.0 all-reduce.4.cloned.1.call-start
  9.7 42.6 %reduce-scatter.2.cloned.1.call-done = bf16[1,256,1536]{2,1,0:T(8,128)(2,1)} async-done(((bf16[1,1024,1536]{2,1,0:T(8,128)(2,1)}), bf16[1,256,1536]{2,1,0:T(8,128)(2,1)}) %reduce-scatter.2.cloned.1.call-update) | async-done | bytes 786448 | tf_op jit(solution)/shard_map/reduce_scatter | solution.py:26
  52.3 2.1 fusion.6
  54.5 39.5 %psum.21 = f32[]{:T(128)} all-reduce(f32[]{:T(128)} %fusion.6), channel_id=1, replica_groups=mesh['expert'=2,'dp'=4,'shard'=4] {'expert','dp','shard'}, use_global_device_ids=true, to_apply=%region_2.0 | all-reduce | flops 1 | bytes 8 | tf_op jit(solution)/shard_map/psum | solution.py:34
  94.6 0.0 all-gather.4.cloned.1.call-done
  94.7 0.0 copy-done.1
  94.7 2.9 fusion.9
  97.6 1.6 convolution_bitcast_fusion.1
  99.2 0.0 all-reduce.4.cloned.1.call-update
  99.3 0.2 all-reduce.6.cloned.1.call-start
  99.5 92.3 %all-reduce.4.cloned.1.call-done = f32[1,384,384]{1,2,0:T(8,128)} async-done(((f32[1,384,384]{1,2,0:T(8,128)}), f32[1,384,384]{1,2,0:T(8,128)}) %all-reduce.4.cloned.1.call-update) | async-done | bytes 589840 | tf_op jit(solution)/shard_map/psum | solution.py:13
  191.8 1.4 copy.13
  193.2 0.1 fusion.19
  193.3 0.0 copy-start.4
  193.3 0.8 copy-done.4
  194.1 11.7 %custom-call.26 = f32[1,128,128]{2,1,0:T(8,128)S(1)} custom-call(f32[1,128,128]{2,1,0:T(8,128)S(1)} %cholesky.192), custom_call_target="Cholesky" | custom-call | tf_op jit(solution)/shard_map/jit(cholesky)/cholesky | solution.py:16
  205.9 9.8 %custom-call.27 = f32[1,1,128,128]{2,3,1,0:T(8,128)S(1)} custom-call(f32[1,1,128,128]{3,2,1,0:T(8,128)S(1)} %get-tuple-element.33), custom_call_target="InvertDiagBlocksLowerTriangular" | custom-call | tf_op jit(solution)/shard_map/jit(cholesky)/cholesky | solution.py:16
  215.7 1.2 constant_dynamic-update-slice_fusion.2
  216.9 1.2 fusion.12
  218.1 11.7 %custom-call.28 = f32[1,128,128]{2,1,0:T(8,128)S(1)} custom-call(f32[1,128,128]{2,1,0:T(8,128)S(1)} %cholesky.196), custom_call_target="Cholesky" | custom-call | tf_op jit(solution)/shard_map/jit(cholesky)/cholesky | solution.py:16
  229.9 10.0 %custom-call.29 = f32[1,1,128,128]{2,3,1,0:T(8,128)S(1)} custom-call(f32[1,1,128,128]{3,2,1,0:T(8,128)S(1)} %get-tuple-element.30), custom_call_target="InvertDiagBlocksLowerTriangular" | custom-call | tf_op jit(solution)/shard_map/jit(cholesky)/cholesky | solution.py:16
  239.9 0.2 fusion.17
  240.1 1.1 fusion.18
  241.2 11.7 %custom-call.30 = f32[1,128,128]{2,1,0:T(8,128)S(1)} custom-call(f32[1,128,128]{2,1,0:T(8,128)S(1)} %fusion.18), custom_call_target="Cholesky" | custom-call | tf_op jit(solution)/shard_map/jit(cholesky)/cholesky | solution.py:16
  252.9 0.7 compare_reduce_fusion
  253.7 0.6 compare_reduce_fusion.1
  256.3 0.9 select_select_fusion
  257.2 9.0 %while.1 = (s32[]{:T(128)}, f32[1,384,384]{2,1,0:T(8,128)}, s32[3,2]{0,1:T(2,128)S(1)}, f32[3,1,128,128]{3,2,1,0:T(8,128)S(1)}, s32[]{:T(128)}) while((s32[]{:T(128)}, f32[1,384,384]{2,1,0:T(8,128)}, s32[3,2]{0,1:T(2,128)S(1)}, f32[3,1,128,128]{3,2,1,0:T(8,128)S(1)}, s32[]{:T(128)}) %tuple.31), condition=%wide.while_cond, body=%wide.while_body.sunk | while | flops 2 | bytes 131189 | solution.py:19
  257.2 0.1 constant_dynamic-slice_fusion.2
  257.2 0.6 fusion.45
  257.8 2.3 bitcast_dynamic-update-slice_fusion.2
  260.2 0.1 constant_dynamic-slice_fusion.2
  260.3 0.6 fusion.45
  260.9 2.3 bitcast_dynamic-update-slice_fusion.2
  263.2 0.1 constant_dynamic-slice_fusion.2
  263.3 0.6 fusion.45
  263.9 2.3 bitcast_dynamic-update-slice_fusion.2
  266.2 29.5 %custom-call.31 = f32[1,3,128,128]{2,3,1,0:T(8,128)S(1)} custom-call(f32[1,3,128,128]{3,2,1,0:T(8,128)S(1)} %bitcast.165), custom_call_target="InvertDiagBlocksLowerTriangular" | custom-call | tf_op jit(solution)/shard_map/vmap(jit(_solve_triangular))/triangular_solve | solution.py:19
  295.7 0.3 fusion.29
  296.0 1.2 fusion.14
  297.2 0.3 convolution_bitcast_fusion.4
  297.5 1.5 fusion.16
  299.0 0.3 convolution_bitcast_fusion.3
  299.4 3.5 convolution_bitcast_fusion
  302.9 0.0 all-reduce.6.cloned.1.call-update
  302.9 0.3 all-gather.6.cloned.1.call-start
  303.2 97.9 %all-reduce.6.cloned.1.call-done = f32[1536,1,384]{0,2,1:T(8,128)} async-done(((f32[1536,1,384]{0,2,1:T(8,128)}), f32[1536,1,384]{0,2,1:T(8,128)}) %all-reduce.6.cloned.1.call-update) | async-done | bytes 2359312 | tf_op jit(solution)/shard_map/psum | solution.py:48
  401.1 2.0 multiply_reduce_fusion
  403.2 0.3 copy-done
  403.5 3.7 fusion.3
  407.2 0.0 all-gather.6.cloned.1.call-update
  407.2 0.9 dynamic-slice_multiply_fusion
  408.1 1.7 copy.16
  409.8 5.3 %fusion.2 = f32[1,1,256,1536]{3,2,1,0:T(8,128)} fusion(f32[1536,1,384]{0,2,1:T(8,128)S(1)} %copy-done, bf16[1,256,1536]{2,1,0:T(8,128)(2,1)S(1)} %copy-done.2, f32[]{:T(128)S(6)} %div.15, f32[1,1,256,1536]{3,2,1,0:T(8,128)} %param.4, f32[1,128,256]{2,1,0:T(8,128)S(1)} %convolution_bitcast_fusion.3, f32[1,128,256]{2,1,0:T(8,128)S(1)} %convolution_bitcast_fusion.4, ...), kind=kOutput, calls=%fused_computation.7 | convolution fusion | flops 1814102016 | bytes 6684676 | tf_op jit(solution)/shard_map/emr,fer->emf/dot_general | solution.py:54
  415.1 19.6 %all-gather.6.cloned.1.call-done = bf16[1024,1536]{1,0:T(8,128)(2,1)} async-done(((bf16[256,1536]{1,0:T(8,128)(2,1)}), bf16[1024,1536]{1,0:T(8,128)(2,1)}) %all-gather.6.cloned.1.call-update) | async-done | bytes 3145744 | tf_op jit(solution)/shard_map/all_gather | solution.py:61
  434.7 3.8 copy.36
  (15 shorter events, 0.2 us)
Async XLA Ops:
  8.0 44.3 %reduce-scatter.2.cloned.1.call-start = ((), (), s32[]{:S(2)}) async-start(), calls=%async_computation.1 | async-start | bytes 3932160 | tf_op jit(solution)/shard_map/reduce_scatter | solution.py:26
  8.0 0.9 copy-start.5
  8.1 86.6 %copy-start.1 = (f32[1,1,256,1536]{3,2,1,0:T(8,128)S(1)}, f32[1,1,256,1536]{3,2,1,0:T(8,128)}, u32[]{:S(2)}) copy-start(f32[1,1,256,1536]{3,2,1,0:T(8,128)} %param.4) | copy-start | bytes 4718596
  8.7 85.9 %all-gather.4.cloned.1.call-start = ((), (), s32[]{:S(2)}) async-start(), calls=%async_computation.2 | async-start | bytes 1253376 | tf_op jit(solution)/shard_map/all_gather | solution.py:41
  9.6 182.2 %all-reduce.4.cloned.1.call-start = ((), (), s32[]{:S(2)}) async-start(), calls=%async_computation.3 | async-start | bytes 1179648 | tf_op jit(solution)/shard_map/psum | solution.py:13
  99.3 301.9 %all-reduce.6.cloned.1.call-start = ((), (), s32[]{:S(2)}) async-start(), calls=%async_computation.4 | async-start | bytes 4718592 | tf_op jit(solution)/shard_map/psum | solution.py:48
  191.8 1.4 copy-start.3
  193.3 0.8 copy-start.4
  257.1 42.2 %copy-start.2 = (bf16[1,256,1536]{2,1,0:T(8,128)(2,1)S(1)}, bf16[1,256,1536]{2,1,0:T(8,128)(2,1)}, u32[]{:S(2)}) copy-start(bf16[1,256,1536]{2,1,0:T(8,128)(2,1)} %reduce-scatter.2.cloned.1.call-done) | copy-start | bytes 2359300
  302.9 131.8 %all-gather.6.cloned.1.call-start = ((), (), s32[]{:S(2)}) async-start(), calls=%async_computation.5 | async-start | bytes 3932160 | tf_op jit(solution)/shard_map/all_gather | solution.py:61
  401.1 2.4 copy-start
Sparse Core Ops, SparseCore 0:
  11.3 40.9 reduce-scatter.1
  407.3 27.3 all-gather.5
Sparse Core Ops, SparseCore 1:
  12.1 50.7 all-gather.3
  99.3 92.4 all-reduce.3
  303.0 98.1 all-reduce.5
where the time goes:
time: 447 us; the launch traced here: 446 us
  waiting for transfers between devices  253 us (57%)
  other arithmetic  91.9 us (21%)
  blocking collectives  39.5 us (9%)
  matrix products  24.4 us (5%)
  between operations  18.6 us (4%)
  local copies, waits for them, and re-layouts  17.8 us (4%)
    psum x1, waiting for transfers between devices, shards(): right_factor = lax.psum(right_term, ('dp', 'shard'))  97.9 us
    psum x1, waiting for transfers between devices, orthonormal(): lax.psum(jnp.einsum('emr,ems->ers', projected, projected, precision=highe...  92.3 us
    another operation x10, other arithmetic, orthonormal(): triangles = jnp.linalg.cholesky(gram_matrix)  56.4 us
    reduce_scatter x1, waiting for transfers between devices, shards(): lax.psum_scatter(partial_value, 'dp', scatter_dimension=1, tiled=True)  42.6 us
    psum x1, blocking collectives, shards(): lax.psum(jnp.sum(gradient * gradient), ('expert', 'dp', 'shard'))  39.5 us
    another operation x3, other arithmetic, solve_one(): return jax.scipy.linalg.solve_triangular(triangle, columns.T, lower=True).T  30.4 us
    all_gather x1, waiting for transfers between devices, shards(): weight_update = lax.all_gather(local_update, 'dp', axis=1, tiled=True)  19.6 us
    another operation x9, local copies, waits for them, and re-layouts  8.96 us
  transfers between devices with their start and end apart: 5, of which 4 were waited for; matrix products, arithmetic and copies ran while one was open for 2% of the time, Pallas kernels for 0%

commit v1 on v0

--- a/solution.py
+++ b/solution.py
@@ -45,7 +45,8 @@
     )
     ortho_basis = orthonormal(projected)
     right_term = jnp.einsum("emf,emr->fer", buffer, ortho_basis, precision=highest)
-    right_factor = lax.psum(right_term, ("dp", "shard"))
+    _carry_positions = lambda xin: lax.psum(lax.psum(xin, "shard"), "dp")
+    right_factor = _carry_positions(right_term)
     inverse = lax.rsqrt(jnp.sum(right_factor * right_factor, axis=0) + 1e-06)
     offset = (
         lax.axis_index("dp") * lax.axis_size("shard") + lax.axis_index("shard")

time: 447 us -> 498 us (1.11)
  waiting for transfers between devices: 253 us -> 305 us
    psum x1 -> x2, waiting for transfers between devices: 97.9 us -> 148 us  [shards(): _carry_positions = lambda xin: lax.psum(lax.psum(xin, 'shard'), 'dp')]
  transfers between devices with their start and end apart: 5 -> 6, of which waited for: 4 -> 5; matrix products, arithmetic and copies ran while one was open for 2% -> 2% of each run, Pallas kernels for 0% -> 0%
where the time goes in v1:
time: 498 us; the launch traced here: 497 us
  waiting for transfers between devices  305 us (61%)
  other arithmetic  91.9 us (18%)
  blocking collectives  39.5 us (8%)
  matrix products  24.4 us (5%)
  between operations  18.3 us (4%)
  local copies, waits for them, and re-layouts  17.8 us (4%)
    psum x2, waiting for transfers between devices, shards(): _carry_positions = lambda xin: lax.psum(lax.psum(xin, 'shard'), 'dp')  148 us
    psum x1, waiting for transfers between devices, orthonormal(): lax.psum(jnp.einsum('emr,ems->ers', projected, projected, precision=highe...  92.3 us
    another operation x10, other arithmetic, orthonormal(): triangles = jnp.linalg.cholesky(gram_matrix)  56.4 us
    reduce_scatter x1, waiting for transfers between devices, shards(): lax.psum_scatter(partial_value, 'dp', scatter_dimension=1, tiled=True)  42.6 us
    psum x1, blocking collectives, shards(): lax.psum(jnp.sum(gradient * gradient), ('expert', 'dp', 'shard'))  39.5 us
    another operation x3, other arithmetic, solve_one(): return jax.scipy.linalg.solve_triangular(triangle, columns.T, lower=True).T  30.4 us
    all_gather x1, waiting for transfers between devices, shards(): weight_update = lax.all_gather(local_update, 'dp', axis=1, tiled=True)  20.9 us
  transfers between devices with their start and end apart: 6, of which 5 were waited for; matrix products, arithmetic and copies ran while one was open for 2% of the time, Pallas kernels for 0%

profile of v1, /device:TPU:0, one launch (start us, length us, event | category | flops | bytes accessed | tf_op | source)
XLA Modules:
  0.0 497.3 jit_solution(8432761840672657679)
XLA Ops:
  8.0 0.0 reduce-scatter.2.cloned.1.call-start
  8.1 0.0 copy-start.1
  8.1 0.7 reduce-scatter.2.cloned.1.call-update
  8.7 0.0 all-gather.4.cloned.1.call-start
  8.8 0.2 copy-done.5
  9.0 0.6 copy.21
  9.6 0.0 all-gather.4.cloned.1.call-update
  9.6 0.0 all-reduce.5.cloned.1.call-start
  9.7 42.6 %reduce-scatter.2.cloned.1.call-done = bf16[1,256,1536]{2,1,0:T(8,128)(2,1)} async-done(((bf16[1,1024,1536]{2,1,0:T(8,128)(2,1)}), bf16[1,256,1536]{2,1,0:T(8,128)(2,1)}) %reduce-scatter.2.cloned.1.call-update) | async-done | bytes 786448 | tf_op jit(solution)/shard_map/reduce_scatter | solution.py:26
  52.3 2.1 fusion.6
  54.5 39.5 %psum.28 = f32[]{:T(128)} all-reduce(f32[]{:T(128)} %fusion.6), channel_id=1, replica_groups=mesh['expert'=2,'dp'=4,'shard'=4] {'expert','dp','shard'}, use_global_device_ids=true, to_apply=%region_2.0 | all-reduce | flops 1 | bytes 8 | tf_op jit(solution)/shard_map/psum | solution.py:34
  94.6 0.0 all-gather.4.cloned.1.call-done
  94.7 2.9 fusion.9
  97.6 1.6 convolution_bitcast_fusion.1
  99.2 0.0 all-reduce.5.cloned.1.call-update
  99.3 0.2 all-reduce.7.cloned.1.call-start
  99.5 92.3 %all-reduce.5.cloned.1.call-done = f32[1,384,384]{1,2,0:T(8,128)} async-done(((f32[1,384,384]{1,2,0:T(8,128)}), f32[1,384,384]{1,2,0:T(8,128)}) %all-reduce.5.cloned.1.call-update) | async-done | bytes 589840 | tf_op jit(solution)/shard_map/psum | solution.py:13
  191.9 1.4 copy.13
  193.2 0.1 fusion.19
  193.3 0.8 copy-done.4
  194.1 11.7 %custom-call.26 = f32[1,128,128]{2,1,0:T(8,128)S(1)} custom-call(f32[1,128,128]{2,1,0:T(8,128)S(1)} %cholesky.192), custom_call_target="Cholesky" | custom-call | tf_op jit(solution)/shard_map/jit(cholesky)/cholesky | solution.py:16
  205.9 9.8 %custom-call.27 = f32[1,1,128,128]{2,3,1,0:T(8,128)S(1)} custom-call(f32[1,1,128,128]{3,2,1,0:T(8,128)S(1)} %get-tuple-element.33), custom_call_target="InvertDiagBlocksLowerTriangular" | custom-call | tf_op jit(solution)/shard_map/jit(cholesky)/cholesky | solution.py:16
  215.7 1.2 constant_dynamic-update-slice_fusion.2
  216.9 1.2 fusion.12
  218.1 11.7 %custom-call.28 = f32[1,128,128]{2,1,0:T(8,128)S(1)} custom-call(f32[1,128,128]{2,1,0:T(8,128)S(1)} %cholesky.196), custom_call_target="Cholesky" | custom-call | tf_op jit(solution)/shard_map/jit(cholesky)/cholesky | solution.py:16
  229.9 10.0 %custom-call.29 = f32[1,1,128,128]{2,3,1,0:T(8,128)S(1)} custom-call(f32[1,1,128,128]{3,2,1,0:T(8,128)S(1)} %get-tuple-element.30), custom_call_target="InvertDiagBlocksLowerTriangular" | custom-call | tf_op jit(solution)/shard_map/jit(cholesky)/cholesky | solution.py:16
  239.9 0.2 fusion.17
  240.1 1.1 fusion.18
  241.2 11.7 %custom-call.30 = f32[1,128,128]{2,1,0:T(8,128)S(1)} custom-call(f32[1,128,128]{2,1,0:T(8,128)S(1)} %fusion.18), custom_call_target="Cholesky" | custom-call | tf_op jit(solution)/shard_map/jit(cholesky)/cholesky | solution.py:16
  252.9 0.7 compare_reduce_fusion
  253.7 0.6 compare_reduce_fusion.1
  256.3 0.9 select_select_fusion
  257.2 9.0 %while.1 = (s32[]{:T(128)}, f32[1,384,384]{2,1,0:T(8,128)}, s32[3,2]{0,1:T(2,128)S(1)}, f32[3,1,128,128]{3,2,1,0:T(8,128)S(1)}, s32[]{:T(128)}) while((s32[]{:T(128)}, f32[1,384,384]{2,1,0:T(8,128)}, s32[3,2]{0,1:T(2,128)S(1)}, f32[3,1,128,128]{3,2,1,0:T(8,128)S(1)}, s32[]{:T(128)}) %tuple.31), condition=%wide.while_cond, body=%wide.while_body.sunk | while | flops 2 | bytes 131189 | solution.py:19
  257.2 0.1 constant_dynamic-slice_fusion.2
  257.2 0.6 fusion.45
  257.8 2.3 bitcast_dynamic-update-slice_fusion.2
  260.2 0.1 constant_dynamic-slice_fusion.2
  260.3 0.6 fusion.45
  260.9 2.3 bitcast_dynamic-update-slice_fusion.2
  263.2 0.1 constant_dynamic-slice_fusion.2
  263.3 0.6 fusion.45
  263.9 2.3 bitcast_dynamic-update-slice_fusion.2
  266.2 29.5 %custom-call.31 = f32[1,3,128,128]{2,3,1,0:T(8,128)S(1)} custom-call(f32[1,3,128,128]{3,2,1,0:T(8,128)S(1)} %bitcast.165), custom_call_target="InvertDiagBlocksLowerTriangular" | custom-call | tf_op jit(solution)/shard_map/vmap(jit(_solve_triangular))/triangular_solve | solution.py:19
  295.7 0.3 fusion.29
  296.0 1.2 fusion.14
  297.2 0.3 convolution_bitcast_fusion.4
  297.5 1.5 fusion.16
  299.1 0.3 convolution_bitcast_fusion.3
  299.4 3.5 convolution_bitcast_fusion
  302.9 0.0 all-reduce.7.cloned.1.call-update
  302.9 0.0 all-reduce.9.cloned.1.call-start
  303.0 93.6 %all-reduce.7.cloned.1.call-done = f32[1536,1,384]{0,2,1:T(8,128)} async-done(((f32[1536,1,384]{0,2,1:T(8,128)}), f32[1536,1,384]{0,2,1:T(8,128)}) %all-reduce.7.cloned.1.call-update) | async-done | bytes 2359312 | tf_op jit(solution)/shard_map/psum | solution.py:48
  396.5 0.0 all-reduce.9.cloned.1.call-update
  396.6 0.3 all-gather.6.cloned.1.call-start
  396.9 54.5 %all-reduce.9.cloned.1.call-done = f32[1536,1,384]{0,2,1:T(8,128)} async-done(((f32[1536,1,384]{0,2,1:T(8,128)}), f32[1536,1,384]{0,2,1:T(8,128)}) %all-reduce.9.cloned.1.call-update) | async-done | bytes 2359312 | tf_op jit(solution)/shard_map/psum | solution.py:48
  451.4 2.0 multiply_reduce_fusion
  453.5 0.3 copy-done
  453.8 3.7 fusion.3
  457.5 0.0 all-gather.6.cloned.1.call-update
  457.5 0.9 dynamic-slice_multiply_fusion
  458.3 1.7 copy.16
  460.1 5.3 %fusion.2 = f32[1,1,256,1536]{3,2,1,0:T(8,128)} fusion(f32[1536,1,384]{0,2,1:T(8,128)S(1)} %copy-done, bf16[1,256,1536]{2,1,0:T(8,128)(2,1)S(1)} %copy-done.2, f32[]{:T(128)S(6)} %div.15, f32[1,1,256,1536]{3,2,1,0:T(8,128)} %param.4, f32[1,128,256]{2,1,0:T(8,128)S(1)} %convolution_bitcast_fusion.3, f32[1,128,256]{2,1,0:T(8,128)S(1)} %convolution_bitcast_fusion.4, ...), kind=kOutput, calls=%fused_computation.7 | convolution fusion | flops 1814102016 | bytes 6684676 | tf_op jit(solution)/shard_map/emr,fer->emf/dot_general | solution.py:55
  465.4 20.9 %all-gather.6.cloned.1.call-done = bf16[1024,1536]{1,0:T(8,128)(2,1)} async-done(((bf16[256,1536]{1,0:T(8,128)(2,1)}), bf16[1024,1536]{1,0:T(8,128)(2,1)}) %all-gather.6.cloned.1.call-update) | async-done | bytes 3145744 | tf_op jit(solution)/shard_map/all_gather | solution.py:62
  486.2 3.8 copy.37
  (18 shorter events, 0.2 us)
Async XLA Ops:
  8.0 44.3 %reduce-scatter.2.cloned.1.call-start = ((), (), s32[]{:S(2)}) async-start(), calls=%async_computation.1 | async-start | bytes 3932160 | tf_op jit(solution)/shard_map/reduce_scatter | solution.py:26
  8.0 0.9 copy-start.5
  8.1 86.6 %copy-start.1 = (f32[1,1,256,1536]{3,2,1,0:T(8,128)S(1)}, f32[1,1,256,1536]{3,2,1,0:T(8,128)}, u32[]{:S(2)}) copy-start(f32[1,1,256,1536]{3,2,1,0:T(8,128)} %param.4) | copy-start | bytes 4718596
  8.7 85.9 %all-gather.4.cloned.1.call-start = ((), (), s32[]{:S(2)}) async-start(), calls=%async_computation.2 | async-start | bytes 1253376 | tf_op jit(solution)/shard_map/all_gather | solution.py:41
  9.6 182.2 %all-reduce.5.cloned.1.call-start = ((), (), s32[]{:S(2)}) async-start(), calls=%async_computation.3 | async-start | bytes 1179648 | tf_op jit(solution)/shard_map/psum | solution.py:13
  99.3 297.3 %all-reduce.7.cloned.1.call-start = ((), (), s32[]{:S(2)}) async-start(), calls=%async_computation.4 | async-start | bytes 4718592 | tf_op jit(solution)/shard_map/psum | solution.py:48
  191.9 1.4 copy-start.3
  193.3 0.8 copy-start.4
  257.2 42.2 %copy-start.2 = (bf16[1,256,1536]{2,1,0:T(8,128)(2,1)S(1)}, bf16[1,256,1536]{2,1,0:T(8,128)(2,1)}, u32[]{:S(2)}) copy-start(bf16[1,256,1536]{2,1,0:T(8,128)(2,1)} %reduce-scatter.2.cloned.1.call-done) | copy-start | bytes 2359300
  302.9 148.5 %all-reduce.9.cloned.1.call-start = ((), (), s32[]{:S(2)}) async-start(), calls=%async_computation.5 | async-start | bytes 4718592 | tf_op jit(solution)/shard_map/psum | solution.py:48
  396.6 89.7 %all-gather.6.cloned.1.call-start = ((), (), s32[]{:S(2)}) async-start(), calls=%async_computation.6 | async-start | bytes 3932160 | tf_op jit(solution)/shard_map/all_gather | solution.py:62
  451.4 2.4 copy-start
Sparse Core Ops, SparseCore 0:
  11.3 40.9 reduce-scatter.1
  396.7 54.6 all-reduce.8
  457.6 28.5 all-gather.5
Sparse Core Ops, SparseCore 1:
  12.1 50.7 all-gather.3
  99.3 92.4 all-reduce.4
  303.0 93.5 all-reduce.6
